TPU v7x, 768 devices: a whole 4x8x12 slice. The times are simulated.
768 devices in a mesh: grp: 48 (over z, x), row: 16 (over y, core).
Axes of the slice: x: 4, y: 8, z: 12, core: 2. Of those that a mesh axis runs over, the one named last changes fastest.
Arguments:
- gll_state: float32 [8, 32, 16, 98304], P(None, None, None, ('grp', 'row')), may hold values from -6 to 6
- metric: float32 [16, 98304], P(None, ('grp', 'row')), may hold values from 0.7 to 1.4
- phys_owner: int32 [98304, 4, 1], P(('grp', 'row')), may hold values from 0 to 47; in each aligned block of 512 rows (0 to 511, 512 to 1023, ..., all dimensions but the last counted through in order) at most 22 rows name the same one
- neighbours: int32 [4, 98304], P(None, ('grp', 'row')), may hold values from 0 to 98303, as said below
- phys_rate: float32 [32, 811008], P(None, ('grp', 'row')), may hold values from 0.2 to 2
- phys_forcing: float32 [32, 811008], P(None, ('grp', 'row')), may hold values from -6 to 6
- field_mix: float32 [8, 8], replicated, may hold values from -2 to 2
Outputs:
- gll_tend: float32 [8, 32, 16, 98304], P(None, None, None, ('grp', 'row'))
Inputs may be any that keep to these rules, and one draw needn't show every extreme that they name: `phys_owner`: in the 512 rows of one device, no owner is named more than 22 times, and some owner reaches 22. `neighbours`: rows 0 and 1 of element e are e - 1 and e + 1, cyclically over 98304 elements; rows 2 and 3 lie 2 to 32 positions before and after e, cyclically, and some element has a neighbour exactly 32 positions away.
All inputs are finite; a program needn't handle non-finite values.
Results may differ from a plain program's by a relative error of at most 0.000094.
Values sent between devices are 32-bit elements; how exact they have to be, the bound alone decides.
A program may use at most 32 MiB of HBM per device.

v0:
```python
import jax
import jax.numpy as jnp
import numpy as np
from jax import lax
from jax.sharding import PartitionSpec as P

HALO = 32


def side_by_side(arrays, axis, split_dim, concat_dim, along):
    widths = [a.shape[along] for a in arrays]
    both = jnp.concatenate(arrays, axis=along)
    out = lax.all_to_all(both, axis, split_axis=split_dim, concat_axis=concat_dim, tiled=True)
    return tuple(jnp.split(out, [sum(widths[:k]) for k in range(1, len(widths))], axis=along))


def with_halo(x, sides, width):
    edges = {}
    for axis, dim in sides:
        count, length = (lax.axis_size(axis), x.shape[dim])
        up = [(i, (i + 1) % count) for i in range(count)]
        last = lax.slice_in_dim(x, length - width, length, axis=dim)
        first = lax.slice_in_dim(x, 0, width, axis=dim)
        edges[dim] = (
            lax.ppermute(last, axis, up),
            lax.ppermute(first, axis, [(b, a) for a, b in up]),
        )
    done = []
    for _, dim in sides:
        low, high = edges[dim]
        around = [(width, width) if d in done else (0, 0) for d in range(x.ndim)]
        x = jnp.concatenate([jnp.pad(low, around), x, jnp.pad(high, around)], axis=dim)
        done.append(dim)
    return x


def lagrange_value(gll_nodes, node_index, point):
    value = 1.0
    for other_index in range(4):
        if other_index != node_index:
            value = (
                value
                * (point - gll_nodes[other_index])
                / (gll_nodes[node_index] - gll_nodes[other_index])
            )
    return value


def remap_tables():
    gll_nodes = np.array([-1.0, -1.0 / np.sqrt(5.0), 1.0 / np.sqrt(5.0), 1.0])
    offset = 0.5 / np.sqrt(3.0)
    halves = np.zeros((2, 4))
    for node_index in range(4):
        left_sum = lagrange_value(gll_nodes, node_index, -0.5 - offset) + lagrange_value(
            gll_nodes, node_index, -0.5 + offset
        )
        right_sum = lagrange_value(gll_nodes, node_index, 0.5 - offset) + lagrange_value(
            gll_nodes, node_index, 0.5 + offset
        )
        halves[0, node_index] = 0.5 * left_sum
        halves[1, node_index] = 0.5 * right_sum
    cell_weights = (halves[None, :, None, :] * halves[:, None, :, None]).reshape(4, 16)
    interp_cols = np.stack([0.5 - gll_nodes, 0.5 + gll_nodes], axis=1)
    cell_to_node = (interp_cols[None, :, None, :] * interp_cols[:, None, :, None]).reshape(16, 4)
    node_x = np.tile(gll_nodes, 4)
    node_y = np.repeat(gll_nodes, 4)
    slope_weights = 0.5 * np.stack(
        [
            np.maximum(0.0, -node_x),
            np.maximum(0.0, node_x),
            np.maximum(0.0, -node_y),
            np.maximum(0.0, node_y),
        ],
        axis=1,
    )
    return (
        jnp.asarray(cell_weights, jnp.float32),
        jnp.asarray(cell_to_node, jnp.float32),
        jnp.asarray(slope_weights, jnp.float32),
    )


def to_cells(gll_state, metric):
    cell_weights, cell_to_node, slope_weights = remap_tables()
    weighted = cell_weights[:, :, None] * metric[None, :, :]
    cell_area = jnp.sum(weighted, axis=1)
    cell_mass = jnp.einsum("cne,flne->flce", weighted, gll_state, precision=lax.Precision.HIGHEST)
    return cell_mass / cell_area[None, None]


def physics(cell_values, relax_rate, forcing, field_mix):
    mixed_fields = jnp.einsum(
        "fg,g...->f...", field_mix, cell_values, precision=lax.Precision.HIGHEST
    )
    return relax_rate[None] * jnp.tanh(mixed_fields + forcing[None])


def to_nodes(tendency, neighbour_means):
    cell_weights, cell_to_node, slope_weights = remap_tables()
    own_mean = jnp.mean(tendency, axis=2)
    reconstructed = jnp.einsum(
        "nc,flce->flne", cell_to_node, tendency, precision=lax.Precision.HIGHEST
    )
    reconstructed = reconstructed + jnp.einsum(
        "nk,flke->flne",
        slope_weights,
        neighbour_means - own_mean[:, :, None],
        precision=lax.Precision.HIGHEST,
    )
    lower_bound = jnp.minimum(jnp.min(tendency, axis=2), jnp.min(neighbour_means, axis=2))
    upper_bound = jnp.maximum(jnp.max(tendency, axis=2), jnp.max(neighbour_means, axis=2))
    return jnp.clip(reconstructed, lower_bound[:, :, None], upper_bound[:, :, None])


def on_device(gll_state, metric, phys_owner, neighbours, phys_rate, phys_forcing, field_mix):
    field_count, level_count, node_count, elem_count = gll_state.shape
    grp_size = lax.axis_size("grp")
    row_size = lax.axis_size("row")
    capacity = phys_rate.shape[1] // grp_size
    cell_values = to_cells(gll_state, metric)
    column_cells = cell_values.transpose(0, 1, 3, 2).reshape(
        field_count, level_count, 4 * elem_count
    )
    owner_grp = phys_owner[:, :, 0].reshape(4 * elem_count)
    onehot = (owner_grp[:, None] == jnp.arange(grp_size, dtype=jnp.int32)[None, :]).astype(
        jnp.int32
    )
    slot_rank = jnp.sum((jnp.cumsum(onehot, axis=0) - onehot) * onehot, axis=1)
    target = owner_grp * capacity + slot_rank
    rate_slots, forcing_slots = side_by_side(
        (
            phys_rate.reshape(level_count, grp_size, capacity),
            phys_forcing.reshape(level_count, grp_size, capacity),
        ),
        "grp",
        1,
        1,
        0,
    )
    relax_rate = rate_slots.reshape(level_count, grp_size * capacity)[:, target]
    forcing = forcing_slots.reshape(level_count, grp_size * capacity)[:, target]
    column_tend = physics(column_cells, relax_rate, forcing, field_mix)
    tendency = column_tend.reshape(field_count, level_count, elem_count, 4).transpose(0, 1, 3, 2)
    own_mean = jnp.mean(tendency, axis=2).reshape(field_count * level_count, elem_count)
    padded = with_halo(own_mean, ((("grp", "row"), 1),), HALO)
    total_elems = elem_count * grp_size * row_size
    first_elem = (lax.axis_index("grp") * row_size + lax.axis_index("row")) * elem_count
    local_index = (neighbours - first_elem + HALO) % total_elems
    neighbour_means = jnp.take(padded, local_index, axis=1).reshape(
        field_count, level_count, 4, elem_count
    )
    return to_nodes(tendency, neighbour_means)


def solution(mesh):
    in_specs = (
        P(None, None, None, ("grp", "row")),
        P(None, ("grp", "row")),
        P(("grp", "row"), None, None),
        P(None, ("grp", "row")),
        P(None, ("grp", "row")),
        P(None, ("grp", "row")),
        P(),
    )
    out_specs = P(None, None, None, ("grp", "row"))
    return jax.shard_map(
        on_device, mesh=mesh, in_specs=in_specs, out_specs=out_specs, check_vma=False
    )
```

profile of v0, /device:TPU:64, one launch (start us, length us, event | category | flops | bytes accessed | tf_op | source)
XLA Modules:
  0.0 75.8 jit_solution(14486172956807652560)
XLA Ops:
  0.0 1.4 %reshape.101 = f32[32,48,22]{2,1,0:T(8,128)S(1)} reshape(f32[32,1056]{1,0:T(8,128)} %param.15) | data formatting | bytes 270336 | tf_op jit(solution)/shard_map/reshape | solution.py:133
  1.4 1.3 %reshape.100 = f32[32,48,22]{2,1,0:T(8,128)S(1)} reshape(f32[32,1056]{1,0:T(8,128)} %param.14) | data formatting | bytes 270336 | tf_op jit(solution)/shard_map/reshape | solution.py:132
  2.8 0.7 copy.131
  3.5 1.0 %reshape.140 = f32[48,1,1408]{2,1,0:T(1,128)} reshape(f32[48,22,64]{2,1,0:T(8,128)S(1)} %bitcast.86) | data formatting | bytes 540672
  4.6 17.6 %all-to-all-start = ((f32[48,1,1408]{2,1,0:T(1,128)}), f32[48,1,1408]{2,1,0:T(1,128)S(1)}, u32[]{:S(2)}, u32[]{:S(2)}) async-start(f32[48,1,1408]{2,1,0:T(1,128)} %reshape.140), calls=%async_computation | async-start | bytes 540672 | tf_op jit(solution)/shard_map/all_to_all | solution.py:13
  22.6 8.4 %copy.140 = f32[8,32,16,128]{1,2,0,3:T(8,128)} copy(f32[8,32,16,128]{3,2,1,0:T(8,128)} %param.10) | data formatting | bytes 4194304 | tf_op args[0]
  31.1 0.2 multiply_reduce_fusion
  31.3 6.6 %divide_bitcast_fusion = f32[8,32,128,4]{1,3,0,2:T(4,128)S(1)} fusion(f32[8,32,16,128]{1,2,0,3:T(8,128)} %copy.140, f32[128,4]{1,0:T(8,128)S(1)} %bitcast.93, f32[16,128]{0,1:T(8,128)S(1)} %copy.139, f32[4,16]{1,0:T(4,128)S(1)} %copy-done.6), kind=kOutput, calls=%fused_computation.4 | convolution fusion | flops 25305088 | bytes 2631936 | tf_op jit(solution)/shard_map/cne,flne->flce/dot_general | solution.py:87
  38.1 0.9 %copy.142 = f32[8,32,512]{2,0,1:T(8,128)S(1)} copy(f32[8,32,512]{1,0,2:T(8,128)S(1)} %bitcast.83) | data formatting | bytes 1048576 | tf_op jit(solution)/shard_map/reshape | solution.py:121
  39.2 1.2 %reduce-window.6 = s32[48,4,128]{2,0,1:T(8,128)S(1)} reduce-window(s32[48,4,128]{2,0,1:T(8,128)S(1)} %fusion.11, s32[]{:T(128)} %constant.26.clone.1), window={size=1x1x128 pad=0_0x0_0x127_0}, to_apply=%region_0.0 | reduce-window | flops 3121152 | bytes 196612 | tf_op jit(solution)/shard_map/reduce-window
  40.4 0.2 slice_reduce_fusion
  40.9 0.5 broadcast.97
  41.4 1.3 %reduce.4 = f32[48,1408]{1,0:T(8,128)S(1)} reduce(f32[48,1,1408]{2,1,0:T(1,128)S(1)} %all-to-all-done, f32[]{:T(128)} %broadcast.97), dimensions={1}, to_apply=%all_to_all.3.reduce_sub_computation | reduce | bytes 540676 | tf_op jit(solution)/shard_map/all_to_all | solution.py:13
  42.9 0.2 fusion.14
  43.2 1.0 %gather_fusion.1 = f32[512,32]{1,0:T(8,128)S(1)} fusion(f32[32,1056]{0,1:T(8,128)S(1)} %reshape.138, s32[1024]{0:T(1024)S(1)} %pad_clamp_fusion.1), kind=kCustom, calls=%fused_computation.1 | custom fusion | bytes 133120 | tf_op jit(solution)/shard_map/gather | solution.py:141
  44.4 1.0 %gather_fusion = f32[512,32]{1,0:T(8,128)S(1)} fusion(f32[32,1056]{0,1:T(8,128)S(1)} %reshape.137, s32[1024]{0:T(1024)S(1)} %pad_clamp_fusion.1), kind=kCustom, calls=%fused_computation | custom fusion | bytes 133120 | tf_op jit(solution)/shard_map/gather | solution.py:140
  45.5 0.6 fusion.2
  46.1 0.9 %copy.146 = f32[8,32,512]{1,0,2:T(8,128)S(1)} copy(f32[8,32,512]{2,0,1:T(8,128)S(1)} %fusion.2) | data formatting | bytes 1048576 | tf_op jit(solution)/shard_map/mul | solution.py:95
  47.0 1.7 %bitcast_reduce_fusion.2 = (f32[8,32,128]{1,0,2:T(8,128)S(1)}, f32[8,32,128]{1,0,2:T(8,128)}, f32[8,32,128]{1,0,2:T(8,128)S(1)}) fusion(f32[8,32,512]{1,0,2:T(8,128)S(1)} %copy.146), kind=kLoop, calls=%fused_computation.41 | loop fusion | flops 294912 | bytes 917504 | tf_op jit(solution)/shard_map/reduce_max | solution.py:111
  48.7 2.1 %copy.158 = f32[8,32,4,128]{3,2,1,0:T(4,128)} copy(f32[8,32,4,128]{1,0,2,3:T(8,128)S(1)} %bitcast.82) | data formatting | bytes 1048576 | tf_op jit(solution)/shard_map/transpose | solution.py:143
  50.8 1.2 %copy.147 = f32[8,32,128]{2,1,0:T(8,128)S(1)} copy(f32[8,32,128]{1,0,2:T(8,128)} %get-tuple-element.6) | data formatting | bytes 262144 | tf_op jit(solution)/shard_map/reduce_sum | solution.py:144
  52.2 0.6 fusion.15
  52.8 6.4 %collective-permute-start.1 = (f32[256,32]{0,1:T(8,128)}, f32[256,32]{0,1:T(8,128)}, u32[]{:S(2)}, u32[]{:S(2)}) collective-permute-start(f32[256,32]{0,1:T(8,128)} %get-tuple-element.13), channel_id=1, source_target_pairs={{1,0},{2,1},{3,2},{4,3},{5,4},{6,5},{7,6},{8,7},{9,8},{10,9},{11,1... | collective-permute-start | bytes 98312 | tf_op jit(solution)/shard_map/ppermute | solution.py:26
  59.2 2.1 %collective-permute-start = (f32[256,32]{0,1:T(8,128)}, f32[256,32]{0,1:T(8,128)}, u32[]{:S(2)}, u32[]{:S(2)}) collective-permute-start(f32[256,32]{0,1:T(8,128)} %get-tuple-element.12), channel_id=1, source_target_pairs={{0,1},{1,2},{2,3},{3,4},{4,5},{5,6},{6,7},{7,8},{8,9},{9,10},{10,1... | collective-permute-start | bytes 98312 | tf_op jit(solution)/shard_map/ppermute | solution.py:25
  61.3 2.9 %fusion.16 = f32[8,32,128,16]{2,3,1,0:T(8,128)S(1)} fusion(f32[8,32,4,128]{3,2,1,0:T(4,128)} %copy.158, f32[16,4,1,1]{0,1,3,2:T(4,128)S(1)} %copy-done.7), kind=kOutput, calls=%fused_computation.45 | convolution fusion | flops 25165824 | bytes 2621696 | tf_op jit(solution)/shard_map/nc,flce->flne/dot_general | solution.py:101
  64.2 0.9 %copy.157 = f32[8,32,128]{2,1,0:T(8,128)} copy(f32[8,32,128]{1,0,2:T(8,128)S(1)} %get-tuple-element.7) | data formatting | bytes 262144 | tf_op jit(solution)/shard_map/reduce_min | solution.py:110
  65.3 3.7 %collective-permute-done = f32[256,32]{0,1:T(8,128)} collective-permute-done((f32[256,32]{0,1:T(8,128)}, f32[256,32]{0,1:T(8,128)}, u32[]{:S(2)}, u32[]{:S(2)}) %collective-permute-start) | collective-permute-done | bytes 32800 | tf_op jit(solution)/shard_map/ppermute | solution.py:25
  68.9 0.8 %pad_maximum_fusion.1 = f32[256,192]{0,1:T(8,128)S(1)} fusion(f32[256,32]{0,1:T(8,128)} %collective-permute-done.1, f32[256,128]{0,1:T(8,128)S(1)} %copy.148, f32[256,32]{0,1:T(8,128)} %collective-permute-done), kind=kLoop, calls=%fused_computation.17 | loop fusion | flops 98304 | bytes 393216 | tf_op jit(solution)/shard_map/concatenate | solution.py:32
  69.7 1.6 %gather_fusion.2 = f32[512,256]{1,0:T(8,128)S(1)} fusion(f32[256,192]{0,1:T(8,128)S(1)} %pad_maximum_fusion.1, s32[1024]{0:T(1024)S(1)} %pad_clamp_fusion), kind=kCustom, calls=%fused_computation.2 | custom fusion | bytes 1050624 | tf_op jit(solution)/shard_map/jit(_take)/gather | solution.py:149
  71.3 0.2 copy.151
  71.7 0.6 copy-done.1
  72.3 3.5 %minimum_bitcast_fusion = f32[8,32,16,128]{3,2,1,0:T(8,128)} fusion(f32[8,32,128,16]{2,3,1,0:T(8,128)S(1)} %fusion.16, f32[16,4,1,1]{0,1,3,2:T(4,128)S(1)} %copy-done.5, f32[8,32,128]{2,1,0:T(8,128)S(1)} %min.23, f32[8,32,128]{2,1,0:T(8,128)S(1)} %max.20, f32[8,32,4,128]{3,1,0,2:T(8,128)S(1)} %select_subtract_fusion), kind=kOutput, calls=%fused_computation.3 | convolution fusion | flops 26738688 | bytes 4980992 | tf_op jit(solution)/shard_map/nk,flke->flne/dot_general | solution.py:104
  (47 shorter events, 2.1 us)
Async XLA Ops:
  0.0 45.5 %copy-start = (f32[8,8]{1,0:T(8,128)S(1)}, f32[8,8]{1,0:T(8,128)}, u32[]{:S(2)}) copy-start(f32[8,8]{1,0:T(8,128)} %param.16) | copy-start | bytes 772
  2.8 19.4 %copy-start.3 = (s32[128,4,1]{0,2,1:T(1,128)S(1)}, s32[128,4,1]{0,2,1:T(1,128)}, u32[]{:S(2)}) copy-start(s32[128,4,1]{0,2,1:T(1,128)} %param.12) | copy-start | bytes 6148
  4.6 36.3 %all-to-all-start = ((f32[48,1,1408]{2,1,0:T(1,128)}), f32[48,1,1408]{2,1,0:T(1,128)S(1)}, u32[]{:S(2)}, u32[]{:S(2)}) async-start(f32[48,1,1408]{2,1,0:T(1,128)} %reshape.140), calls=%async_computation | async-start | bytes 540672 | tf_op jit(solution)/shard_map/all_to_all | solution.py:13
  22.6 8.4 %copy-start.2 = (f32[16,128]{1,0:T(8,128)S(1)}, f32[16,128]{1,0:T(8,128)}, u32[]{:S(2)}) copy-start(f32[16,128]{1,0:T(8,128)} %param.11) | copy-start | bytes 24580
  22.6 8.5 %copy-start.6 = (f32[4,16]{1,0:T(4,128)S(1)}, f32[4,16]{1,0:T(4,128)}, u32[]{:S(2)}) copy-start(f32[4,16]{1,0:T(4,128)} %constant.66.clone) | copy-start | bytes 772
  38.1 2.8 %copy-start.4 = (s32[4,128]{1,0:T(4,128)S(1)}, s32[4,128]{1,0:T(4,128)}, u32[]{:S(2)}) copy-start(s32[4,128]{1,0:T(4,128)} %param.13) | copy-start | bytes 6148
  48.7 12.6 %copy-start.7 = (f32[16,4,1,1]{0,1,3,2:T(4,128)S(1)}, f32[16,4,1,1]{0,1,3,2:T(4,128)}, u32[]{:S(2)}) copy-start(f32[16,4,1,1]{0,1,3,2:T(4,128)} %constant.75) | copy-start | bytes 772
  52.8 12.5 %collective-permute-start.1 = (f32[256,32]{0,1:T(8,128)}, f32[256,32]{0,1:T(8,128)}, u32[]{:S(2)}, u32[]{:S(2)}) collective-permute-start(f32[256,32]{0,1:T(8,128)} %get-tuple-element.13), channel_id=1, source_target_pairs={{1,0},{2,1},{3,2},{4,3},{5,4},{6,5},{7,6},{8,7},{9,8},{10,9},{11,1... | collective-permute-start | bytes 98312 | tf_op jit(solution)/shard_map/ppermute | solution.py:26
  59.2 9.8 %collective-permute-start = (f32[256,32]{0,1:T(8,128)}, f32[256,32]{0,1:T(8,128)}, u32[]{:S(2)}, u32[]{:S(2)}) collective-permute-start(f32[256,32]{0,1:T(8,128)} %get-tuple-element.12), channel_id=1, source_target_pairs={{0,1},{1,2},{2,3},{3,4},{4,5},{5,6},{6,7},{7,8},{8,9},{9,10},{10,1... | collective-permute-start | bytes 98312 | tf_op jit(solution)/shard_map/ppermute | solution.py:25
  71.3 0.9 %copy-start.1 = (f32[8,32,128]{2,1,0:T(8,128)S(1)}, f32[8,32,128]{2,1,0:T(8,128)}, u32[]{:S(2)}) copy-start(f32[8,32,128]{2,1,0:T(8,128)} %copy.157) | copy-start | bytes 393220
  71.3 0.9 %copy-start.5 = (f32[16,4,1,1]{0,1,3,2:T(4,128)S(1)}, f32[16,4,1,1]{0,1,3,2:T(4,128)}, u32[]{:S(2)}) copy-start(f32[16,4,1,1]{0,1,3,2:T(4,128)} %constant.76) | copy-start | bytes 772
where the time goes:
time: 76.3 us; the launch traced here: 75.8 us
  local copies, waits for them, and re-layouts  26.4 us (35%)
  starting transfers between devices  26.1 us (34%)
  matrix products  13.6 us (18%)
  other arithmetic  5.69 us (7%)
  waiting for transfers between devices  3.67 us (5%)
    all_to_all x1, starting transfers between devices, side_by_side(): lax.all_to_all(both, axis, split_axis=split_dim, concat_axis=concat_dim,...  17.6 us
    unnamed x21, local copies, waits for them, and re-layouts  10.4 us
    dot_general x1, matrix products, to_cells(): jnp.einsum('cne,flne->flce', weighted, gll_state, precision=lax.Precision...  6.59 us
    ppermute x1, starting transfers between devices, with_halo(): lax.ppermute(first, axis, [(b, a) for a, b in up])  6.36 us
    ppermute x1, waiting for transfers between devices, with_halo(): lax.ppermute(last, axis, up)  3.67 us
    dot_general x1, matrix products, to_nodes(): jnp.einsum('nk,flke->flne', slope_weights, neighbour_means - own_mean[:,...  3.54 us
    dot_general x1, matrix products, to_nodes(): jnp.einsum('nc,flce->flne', cell_to_node, tendency, precision=lax.Precisi...  2.88 us
    ppermute x1, starting transfers between devices, with_halo(): lax.ppermute(last, axis, up)  2.14 us
  transfers between devices with their start and end apart: 3, of which 1 were waited for; matrix products, arithmetic and copies ran while one was open for 30% of the time, Pallas kernels for 0%

commit v1 on v0

v1 whole, which is shorter than its diff:
```python
import functools

import jax
import jax.numpy as jnp
import numpy as np
from jax import lax
from jax.experimental import pallas as pl
from jax.experimental.pallas import tpu as pltpu
from jax.sharding import PartitionSpec as P

MESH = pl.DeviceIdType.MESH
F32 = jnp.float32
BF16 = jnp.bfloat16
HIGH = 11


def lagrange_value(gll_nodes, node_index, point):
    value = 1.0
    for other_index in range(4):
        if other_index != node_index:
            value = (
                value
                * (point - gll_nodes[other_index])
                / (gll_nodes[node_index] - gll_nodes[other_index])
            )
    return value


def cell_weights():
    gll_nodes = np.array([-1.0, -1.0 / np.sqrt(5.0), 1.0 / np.sqrt(5.0), 1.0])
    offset = 0.5 / np.sqrt(3.0)
    halves = np.zeros((2, 4))
    for i in range(4):
        halves[0, i] = 0.5 * (
            lagrange_value(gll_nodes, i, -0.5 - offset)
            + lagrange_value(gll_nodes, i, -0.5 + offset)
        )
        halves[1, i] = 0.5 * (
            lagrange_value(gll_nodes, i, 0.5 - offset) + lagrange_value(gll_nodes, i, 0.5 + offset)
        )
    return (halves[None, :, None, :] * halves[:, None, :, None]).reshape(4, 16)


def exchange_kernel(
    n_grp,
    n_row,
    n_x,
    gll_hbm,
    metric_hbm,
    owner_hbm,
    rate_hbm,
    forcing_hbm,
    mix_hbm,
    tend_ref,
    low_ref,
    high_ref,
    gbuf,
    metric_ref,
    owner_ref,
    rate_ref,
    forcing_ref,
    mix_ref,
    wbuf,
    slots_t,
    send,
    recv,
    rows,
    onehot,
    cells,
    edge_out,
    edge_in,
    in_sem,
    gll_sem,
    send_sem,
    recv_sem,
    edge_send_sem,
    edge_recv_sem,
):
    fields = gll_hbm.shape[0]
    n_z = n_grp // n_x
    me = lax.axis_index("grp")
    my_row = lax.axis_index("row")
    my_z, my_x = me // n_x, me % n_x

    small = [
        pltpu.make_async_copy(src, dst, in_sem.at[k])
        for k, (src, dst) in enumerate(
            (
                (rate_hbm, rate_ref),
                (forcing_hbm, forcing_ref),
                (metric_hbm, metric_ref),
                (owner_hbm, owner_ref),
                (mix_hbm, mix_ref),
            )
        )
    ]
    for copy in small:
        copy.start()
    gll_copies = [
        pltpu.make_async_copy(gll_hbm.at[f], gbuf.at[f], gll_sem.at[f]) for f in range(fields)
    ]
    for copy in gll_copies:
        copy.start()

    here = me * n_row + my_row
    total = n_grp * n_row
    after = lax.rem(here + 1, total)
    before = lax.rem(here + total - 1, total)
    sides = [(d // n_row, d % n_row) for d in (before, after)]

    def partner(i):
        m = i // n_x
        half = (m + 1) // 2
        dz = n_z // 2 + half * (1 - 2 * (m % 2))
        dx = n_x - 1 - i % n_x
        there = ((my_z + dz) % n_z) * n_x + (my_x + dx) % n_x
        origin = ((my_z - dz + n_z) % n_z) * n_x + (my_x - dx + n_x) % n_x
        return there, origin

    barrier = pltpu.get_barrier_semaphore()

    def greet(i, carry):
        there, _ = partner(i)
        pl.semaphore_signal(barrier, inc=1, device_id=(there, my_row), device_id_type=MESH)
        return carry

    for side in sides:
        pl.semaphore_signal(barrier, inc=1, device_id=side, device_id_type=MESH)
    lax.fori_loop(0, n_grp - 1, greet, 0)

    small[0].wait()
    small[1].wait()
    slot_count = rate_ref.shape[1]
    for k in range(0, slot_count, 128):
        width = min(128, slot_count - k)
        r = rate_ref[:, k : k + width]
        f = forcing_ref[:, k : k + width]
        slots_t[k : k + width, :] = jnp.concatenate([r, f, r, f], axis=0).T
    lane = lax.broadcasted_iota(jnp.int32, (HIGH, 128), 1)
    for g in range(n_grp):
        at = 2 * HIGH * g
        send[g] = jnp.where(lane < 64, slots_t[at : at + HIGH], slots_t[at + HIGH : at + 2 * HIGH])

    small[2].wait()
    table = cell_weights()
    for c in range(4):
        weighted = [metric_ref[n : n + 1, :] * float(table[c, n]) for n in range(16)]
        area = functools.reduce(lambda a, b: a + b, weighted)
        inverse = 1.0 / area
        for n in range(16):
            wbuf[16 * c + n : 16 * c + n + 1, :] = weighted[n] * inverse

    levels = tend_ref.shape[2]
    for copy in gll_copies:
        copy.wait()

    def to_cells(f, carry):
        sums = [None] * 4
        for n in range(16):
            g = gbuf[f, pl.ds(n, levels, stride=16), :]
            for c in range(4):
                term = wbuf[16 * c + n : 16 * c + n + 1, :] * g
                sums[c] = term if sums[c] is None else sums[c] + term
        for c in range(4):
            cells[f, c] = sums[c]
        return carry

    lax.fori_loop(0, fields, to_cells, 0)

    pl.semaphore_wait(barrier, n_grp + 1)

    def block_copy(i):
        there, _ = partner(i)
        return pltpu.make_async_remote_copy(
            src_ref=send.at[there],
            dst_ref=recv.at[me],
            send_sem=send_sem.at[i],
            recv_sem=recv_sem.at[i],
            device_id=(there, my_row),
            device_id_type=MESH,
        )

    def start_block(i, carry):
        block_copy(i).start()
        return carry

    lax.fori_loop(0, n_grp - 1, start_block, 0)

    small[4].wait()

    def mix(i, carry):
        c, at = i // (levels // 8), pl.multiple_of((i % (levels // 8)) * 8, 8)
        block = [cells[g, c, pl.ds(at, 8), :] for g in range(fields)]
        for f in range(fields):
            total_f = mix_ref[f, 0] * block[0]
            for g in range(1, fields):
                total_f = total_f + mix_ref[f, g] * block[g]
            cells[f, c, pl.ds(at, 8), :] = total_f
        return carry

    lax.fori_loop(0, 4 * (levels // 8), mix, 0)

    small[3].wait()
    grp_ids = lax.broadcasted_iota(jnp.int32, (n_grp, 128), 0)
    owners = [owner_ref[c : c + 1, :] for c in range(4)]
    match = [jnp.where(grp_ids == owners[c], 1.0, 0.0).astype(F32) for c in range(4)]
    count = match[0] + match[1] + match[2] + match[3]
    before_e = lax.broadcasted_iota(jnp.int32, (128, 128), 0) < lax.broadcasted_iota(
        jnp.int32, (128, 128), 1
    )
    running = jnp.dot(
        count.astype(BF16),
        jnp.where(before_e, 1.0, 0.0).astype(BF16),
        preferred_element_type=F32,
    )
    upper = []
    row_ids = lax.broadcasted_iota(jnp.int32, (256, 128), 0)
    for c in range(4):
        rank = jnp.sum(match[c] * running, axis=0, keepdims=True).astype(jnp.int32)
        running = running + match[c]
        is_upper = rank >= HIGH
        upper.append(is_upper)
        key = owners[c] * 16 + jnp.where(is_upper, rank - HIGH, rank)
        for k in range(n_grp * 16 // 256):
            onehot[256 * k : 256 * k + 256, 128 * c : 128 * c + 128] = jnp.where(
                row_ids == key - 256 * k, 1.0, 0.0
            ).astype(BF16)

    rows[...] = jnp.zeros_like(rows)
    recv[me] = send[me]

    def land(i, carry):
        block_copy(i).wait_recv()
        return carry

    lax.fori_loop(0, n_grp - 1, land, 0)
    for g in range(n_grp):
        rows[16 * g : 16 * g + HIGH, :] = recv[g]

    picked = None
    for k in range(n_grp * 16 // 256):
        block = rows[256 * k : 256 * k + 256, :].T
        top = block.astype(BF16)
        rest = (block - top.astype(F32)).astype(BF16)
        hot = onehot[256 * k : 256 * k + 256, :]
        part = jnp.dot(top, hot, preferred_element_type=F32) + jnp.dot(
            rest, hot, preferred_element_type=F32
        )
        picked = part if picked is None else picked + part

    for c in range(4):
        cut = picked[:, 128 * c : 128 * c + 128]
        both = jnp.where(upper[c], cut[64:128], cut[0:64])
        for f in range(fields):
            tend_ref[f, c] = both[:levels] * jnp.tanh(cells[f, c] + both[levels:])

    lanes = lax.broadcasted_iota(jnp.int32, (levels, 128), 1)
    for half in range(2):
        first, last = None, None
        for q in range(fields // 2):
            f = 2 * q + half
            mean = 0.25 * ((tend_ref[f, 0] + tend_ref[f, 1]) + (tend_ref[f, 2] + tend_ref[f, 3]))
            inside = (lanes >= 32 * q) & (lanes < 32 * q + 32)
            low = pltpu.roll(mean, 32 * q, 1) if q else mean
            high = pltpu.roll(mean, (32 * q + 32) % 128, 1) if (32 * q + 32) % 128 else mean
            first = low if first is None else jnp.where(inside, low, first)
            last = high if last is None else jnp.where(inside, high, last)
        edge_out[0, half * levels : half * levels + levels, :] = first
        edge_out[1, half * levels : half * levels + levels, :] = last

    edge_copies = [
        pltpu.make_async_remote_copy(
            src_ref=edge_out.at[k],
            dst_ref=edge_in.at[1 - k],
            send_sem=edge_send_sem.at[k],
            recv_sem=edge_recv_sem.at[k],
            device_id=sides[k],
            device_id_type=MESH,
        )
        for k in range(2)
    ]
    for copy in edge_copies:
        copy.start()

    def sent(i, carry):
        block_copy(i).wait_send()
        return carry

    lax.fori_loop(0, n_grp - 1, sent, 0)
    for copy in edge_copies:
        copy.wait()
    low_ref[...] = edge_in[0]
    high_ref[...] = edge_in[1]


def nodes_kernel(elems_total, n_row, tend_ref, low_ref, high_ref, near_ref, out_ref, scratch):
    q = pl.program_id(0)
    levels, width = tend_ref.shape[2], tend_ref.shape[3]
    here = (lax.axis_index("grp") * n_row + lax.axis_index("row")) * width
    elem = lax.broadcasted_iota(jnp.int32, (4, width), 1)
    away = near_ref[...] - (here + elem)
    away = jnp.where(away > elems_total // 2, away - elems_total, away)
    away = jnp.where(away < -(elems_total // 2), away + elems_total, away)
    place = elem + away
    inner = jnp.clip(place, 0, width - 1)
    outer = jnp.where(place < 0, place + 32, place - width) + 32 * q
    outer = jnp.clip(outer, 0, width - 1)
    inside = (place >= 0) & (place < width)

    def pick(values, index):
        return jnp.take_along_axis(values, index, axis=1, mode="promise_in_bounds")

    sub = lax.broadcasted_iota(jnp.int32, (8, width), 0)
    g1 = float(1.0 / np.sqrt(5.0))
    i_of = sub % 4
    g_i = jnp.where(i_of == 0, -1.0, jnp.where(i_of == 1, -g1, jnp.where(i_of == 2, g1, 1.0)))
    west_side = i_of < 2
    g_south = jnp.where(sub < 4, -1.0, -g1)
    g_north = jnp.where(sub < 4, g1, 1.0)

    for h in range(2):
        for b in range(levels // 8):
            at = slice(8 * b, 8 * b + 8)
            t = [tend_ref[h, c, at, :] for c in range(4)]
            mean = 0.25 * ((t[0] + t[1]) + (t[2] + t[3]))
            near = []
            halo_at = slice(h * levels + 8 * b, h * levels + 8 * b + 8)
            for k in range(4):
                halo = (low_ref if k % 2 == 0 else high_ref)[halo_at, :]
                own_pick = pick(mean, jnp.broadcast_to(inner[k : k + 1], (8, width)))
                halo_pick = pick(halo, jnp.broadcast_to(outer[k : k + 1], (8, width)))
                near.append(
                    jnp.where(jnp.broadcast_to(inside[k : k + 1], (8, width)), own_pick, halo_pick)
                )
            low = functools.reduce(jnp.minimum, t + near)
            high = functools.reduce(jnp.maximum, t + near)
            slope_x = 0.5 * ((t[1] + t[3]) - (t[0] + t[2]))
            slope_y = 0.5 * ((t[2] + t[3]) - (t[0] + t[1]))
            cross = (t[3] - t[2]) - (t[1] - t[0])
            scratch[0, at, :] = mean
            scratch[1, at, :] = slope_x - 0.5 * (near[0] - mean)
            scratch[2, at, :] = slope_x + 0.5 * (near[1] - mean)
            scratch[3, at, :] = slope_y - 0.5 * (near[2] - mean)
            scratch[4, at, :] = slope_y + 0.5 * (near[3] - mean)
            scratch[5, at, :] = cross
            scratch[6, at, :] = low
            scratch[7, at, :] = high
        for l in range(levels):
            mean, x_west, x_east, y_south, y_north, cross, low, high = (
                jnp.broadcast_to(scratch[k, l : l + 1, :], (8, width)) for k in range(8)
            )
            base = mean + g_i * jnp.where(west_side, x_west, x_east)
            twist = g_i * cross
            out_ref[h, l, 0:8, :] = jnp.minimum(
                jnp.maximum(base + g_south * (y_south + twist), low), high
            )
            out_ref[h, l, 8:16, :] = jnp.minimum(
                jnp.maximum(base + g_north * (y_north + twist), low), high
            )


def on_device(n_grp, n_row, n_x, gll_state, metric, phys_owner, neighbours, rate, forcing, mix):
    fields, levels, nodes, elems = gll_state.shape
    slots = rate.shape[1]
    hbm = pl.BlockSpec(memory_space=pl.ANY)
    vmem = pl.BlockSpec(memory_space=pltpu.VMEM)
    tend, low, high = pl.pallas_call(
        functools.partial(exchange_kernel, n_grp, n_row, n_x),
        out_shape=(
            jax.ShapeDtypeStruct((fields, 4, levels, elems), F32),
            jax.ShapeDtypeStruct((2 * levels, elems), F32),
            jax.ShapeDtypeStruct((2 * levels, elems), F32),
        ),
        in_specs=[hbm] * 6,
        out_specs=(vmem, vmem, vmem),
        scratch_shapes=[
            pltpu.VMEM((fields, levels * nodes, elems), F32),
            pltpu.VMEM((nodes, elems), F32),
            pltpu.VMEM((4, elems), jnp.int32),
            pltpu.VMEM((levels, slots), F32),
            pltpu.VMEM((levels, slots), F32),
            pltpu.SMEM((fields, fields), F32),
            pltpu.VMEM((64, elems), F32),
            pltpu.VMEM((slots, 128), F32),
            pltpu.VMEM((n_grp, HIGH, 128), F32),
            pltpu.VMEM((n_grp, HIGH, 128), F32),
            pltpu.VMEM((n_grp * 16, 128), F32),
            pltpu.VMEM((n_grp * 16, 4 * elems), BF16),
            pltpu.VMEM((fields, 4, levels, elems), F32),
            pltpu.VMEM((2, 2 * levels, elems), F32),
            pltpu.VMEM((2, 2 * levels, elems), F32),
            pltpu.SemaphoreType.DMA((5,)),
            pltpu.SemaphoreType.DMA((fields,)),
            pltpu.SemaphoreType.DMA((n_grp - 1,)),
            pltpu.SemaphoreType.DMA((n_grp - 1,)),
            pltpu.SemaphoreType.DMA((2,)),
            pltpu.SemaphoreType.DMA((2,)),
        ],
        compiler_params=pltpu.CompilerParams(collective_id=0, has_side_effects=True),
        name="exchange",
    )(
        gll_state.reshape(fields, levels * nodes, elems),
        metric,
        phys_owner[:, :, 0].T,
        rate,
        forcing,
        mix,
    )
    return pl.pallas_call(
        functools.partial(nodes_kernel, elems * n_grp * n_row, n_row),
        grid=(fields // 2,),
        out_shape=jax.ShapeDtypeStruct(gll_state.shape, F32),
        in_specs=[
            pl.BlockSpec((2, 4, levels, elems), lambda i: (i, 0, 0, 0)),
            pl.BlockSpec((2 * levels, elems), lambda i: (0, 0)),
            pl.BlockSpec((2 * levels, elems), lambda i: (0, 0)),
            pl.BlockSpec((4, elems), lambda i: (0, 0)),
        ],
        out_specs=pl.BlockSpec((2, levels, nodes, elems), lambda i: (i, 0, 0, 0)),
        scratch_shapes=[pltpu.VMEM((8, levels, elems), F32)],
        name="nodes",
    )(tend, low, high, neighbours)


def solution(mesh):
    in_specs = (
        P(None, None, None, ("grp", "row")),
        P(None, ("grp", "row")),
        P(("grp", "row"), None, None),
        P(None, ("grp", "row")),
        P(None, ("grp", "row")),
        P(None, ("grp", "row")),
        P(),
    )
    out_specs = P(None, None, None, ("grp", "row"))
    n_grp, n_row = mesh.shape["grp"], mesh.shape["row"]
    return jax.shard_map(
        functools.partial(on_device, n_grp, n_row, 4),
        mesh=mesh,
        in_specs=in_specs,
        out_specs=out_specs,
        check_vma=False,
    )
```

time: 76.3 us -> 39.9 us (0.52)
  the two profiles are of different devices: /device:TPU:64 before, /device:TPU:25 now
where the time goes in v1:
time: 39.9 us; the launch traced here: 39.7 us
  Pallas kernels  39.7 us (99%)
    pallas_call x1, Pallas kernels, on_device(): pl.pallas_call(functools.partial(exchange_kernel, n_grp, n_row, n_x), out...  35.6 us
    pallas_call x1, Pallas kernels, on_device(): pl.pallas_call(functools.partial(nodes_kernel, elems * n_grp * n_row, n_r...  4.06 us

profile of v1, /device:TPU:25, one launch (start us, length us, event | category | flops | bytes accessed | tf_op | source)
XLA Modules:
  0.0 39.7 jit_solution(4704386386300702905)
XLA Ops:
  0.0 35.6 %exchange.1 = (f32[8,4,32,128]{3,2,1,0:T(8,128)}, f32[64,128]{1,0:T(8,128)}, f32[64,128]{1,0:T(8,128)}) custom-call(f32[8,512,128]{2,1,0:T(8,128)} %bitcast.4, f32[16,128]{1,0:T(8,128)} %metric_hbm.1, s32[4,128]{1,0:T(4,128)} %bitcast.5, f32[32,1056]{1,0:T(8,128)} %rate_hbm.1, f32[32,1056]{1,0:T(8,128)} %forcing_hbm.1, f32[8,8]{1,0:T(8,128)} %mix_hbm.1), custom_call_target="tpu_custom_call" | custom-call | tf_op jit(solution)/shard_map/exchange/pallas_call | solution.py:367
  35.6 4.1 %nodes.1 = f32[8,32,16,128]{3,2,1,0:T(8,128)} custom-call(f32[8,4,32,128]{3,2,1,0:T(8,128)} %get-tuple-element.8.tend_ref, f32[64,128]{1,0:T(8,128)} %get-tuple-element.9.low_ref, f32[64,128]{1,0:T(8,128)} %get-tuple-element.10.high_ref, s32[4,128]{1,0:T(4,128)} %near_ref.1), custom_call_target="tpu_custom_call" | custom-call | tf_op jit(solution)/shard_map/nodes/pallas_call | solution.py:409

commit v2 on v1

--- a/solution.py
+++ b/solution.py
@@ -44,7 +44,6 @@
 def exchange_kernel(
     n_grp,
     n_row,
-    n_x,
     gll_hbm,
     metric_hbm,
     owner_hbm,
@@ -75,12 +74,12 @@
     recv_sem,
     edge_send_sem,
     edge_recv_sem,
+    ready,
+    edge_ready,
 ):
     fields = gll_hbm.shape[0]
-    n_z = n_grp // n_x
     me = lax.axis_index("grp")
     my_row = lax.axis_index("row")
-    my_z, my_x = me // n_x, me % n_x
 
     small = [
         pltpu.make_async_copy(src, dst, in_sem.at[k])
@@ -108,25 +107,21 @@
     before = lax.rem(here + total - 1, total)
     sides = [(d // n_row, d % n_row) for d in (before, after)]
 
-    def partner(i):
-        m = i // n_x
-        half = (m + 1) // 2
-        dz = n_z // 2 + half * (1 - 2 * (m % 2))
-        dx = n_x - 1 - i % n_x
-        there = ((my_z + dz) % n_z) * n_x + (my_x + dx) % n_x
-        origin = ((my_z - dz + n_z) % n_z) * n_x + (my_x - dx + n_x) % n_x
-        return there, origin
-
     barrier = pltpu.get_barrier_semaphore()
 
-    def greet(i, carry):
-        there, _ = partner(i)
-        pl.semaphore_signal(barrier, inc=1, device_id=(there, my_row), device_id_type=MESH)
-        return carry
-
-    for side in sides:
-        pl.semaphore_signal(barrier, inc=1, device_id=side, device_id_type=MESH)
-    lax.fori_loop(0, n_grp - 1, greet, 0)
+    def greet(g, carry):
+        pl.semaphore_signal(barrier, inc=1, device_id=(g, my_row), device_id_type=MESH)
+        return carry
+
+    lax.fori_loop(me + 1, n_grp, greet, 0)
+
+    @pl.when(here < total - 1)
+    def _():
+        pl.semaphore_signal(barrier, inc=1, device_id=sides[1], device_id_type=MESH)
+
+    @pl.when(here == 0)
+    def _():
+        pl.semaphore_signal(barrier, inc=1, device_id=sides[0], device_id_type=MESH)
 
     small[0].wait()
     small[1].wait()
@@ -141,6 +136,42 @@
         at = 2 * HIGH * g
         send[g] = jnp.where(lane < 64, slots_t[at : at + HIGH], slots_t[at + HIGH : at + 2 * HIGH])
 
+    below = jnp.where(here > 0, 1, 0) + jnp.where(here == total - 1, 1, 0)
+
+    @pl.when(here > 0)
+    def _():
+        pl.semaphore_wait(barrier, me + below)
+
+    def block_copy(there, origin):
+        return pltpu.make_async_remote_copy(
+            src_ref=send.at[there],
+            dst_ref=recv.at[me],
+            send_sem=send_sem.at[there],
+            recv_sem=recv_sem.at[origin],
+            device_id=(there, my_row),
+            device_id_type=MESH,
+        )
+
+    def send_down(g, carry):
+        block_copy(g, me).start()
+        return carry
+
+    lax.fori_loop(0, me, send_down, 0)
+
+    def tell(g, carry):
+        pl.semaphore_signal(ready.at[me], inc=1, device_id=(g, my_row), device_id_type=MESH)
+        return carry
+
+    lax.fori_loop(0, me, tell, 0)
+
+    @pl.when(here > 0)
+    def _():
+        pl.semaphore_signal(edge_ready.at[1], inc=1, device_id=sides[0], device_id_type=MESH)
+
+    @pl.when(here == total - 1)
+    def _():
+        pl.semaphore_signal(edge_ready.at[0], inc=1, device_id=sides[1], device_id_type=MESH)
+
     small[2].wait()
     table = cell_weights()
     for c in range(4):
@@ -166,25 +197,6 @@
         return carry
 
     lax.fori_loop(0, fields, to_cells, 0)
-
-    pl.semaphore_wait(barrier, n_grp + 1)
-
-    def block_copy(i):
-        there, _ = partner(i)
-        return pltpu.make_async_remote_copy(
-            src_ref=send.at[there],
-            dst_ref=recv.at[me],
-            send_sem=send_sem.at[i],
-            recv_sem=recv_sem.at[i],
-            device_id=(there, my_row),
-            device_id_type=MESH,
-        )
-
-    def start_block(i, carry):
-        block_copy(i).start()
-        return carry
-
-    lax.fori_loop(0, n_grp - 1, start_block, 0)
 
     small[4].wait()
 
@@ -229,16 +241,22 @@
     rows[...] = jnp.zeros_like(rows)
     recv[me] = send[me]
 
-    def land(i, carry):
-        block_copy(i).wait_recv()
-        return carry
-
-    lax.fori_loop(0, n_grp - 1, land, 0)
-    for g in range(n_grp):
-        rows[16 * g : 16 * g + HIGH, :] = recv[g]
+    def send_up(g, carry):
+        pl.semaphore_wait(ready.at[g], 1)
+        block_copy(g, me).start()
+        return carry
+
+    lax.fori_loop(me + 1, n_grp, send_up, 0)
 
     picked = None
-    for k in range(n_grp * 16 // 256):
+    for k in range(n_grp // 16):
+        for g in range(16 * k, 16 * k + 16):
+
+            @pl.when(g != me)
+            def _():
+                block_copy(me, g).wait_recv()
+
+            rows[16 * g : 16 * g + HIGH, :] = recv[g]
         block = rows[256 * k : 256 * k + 256, :].T
         top = block.astype(BF16)
         rest = (block - top.astype(F32)).astype(BF16)
@@ -279,23 +297,36 @@
         )
         for k in range(2)
     ]
+
+    @pl.when(here == 0)
+    def _():
+        pl.semaphore_wait(edge_ready.at[0], 1)
+
+    @pl.when(here < total - 1)
+    def _():
+        pl.semaphore_wait(edge_ready.at[1], 1)
+
     for copy in edge_copies:
         copy.start()
 
-    def sent(i, carry):
-        block_copy(i).wait_send()
-        return carry
-
-    lax.fori_loop(0, n_grp - 1, sent, 0)
+    def sent(g, carry):
+        @pl.when(g != me)
+        def _():
+            block_copy(g, me).wait_send()
+
+        return carry
+
+    lax.fori_loop(0, n_grp, sent, 0)
     for copy in edge_copies:
         copy.wait()
     low_ref[...] = edge_in[0]
     high_ref[...] = edge_in[1]
 
 
-def nodes_kernel(elems_total, n_row, tend_ref, low_ref, high_ref, near_ref, out_ref, scratch):
-    q = pl.program_id(0)
-    levels, width = tend_ref.shape[2], tend_ref.shape[3]
+def nodes_kernel(
+    elems_total, n_row, tend_ref, low_ref, high_ref, near_ref, out_hbm, done, scratch, sems
+):
+    fields, _, levels, width = tend_ref.shape
     here = (lax.axis_index("grp") * n_row + lax.axis_index("row")) * width
     elem = lax.broadcasted_iota(jnp.int32, (4, width), 1)
     away = near_ref[...] - (here + elem)
@@ -303,9 +334,15 @@
     away = jnp.where(away < -(elems_total // 2), away + elems_total, away)
     place = elem + away
     inner = jnp.clip(place, 0, width - 1)
-    outer = jnp.where(place < 0, place + 32, place - width) + 32 * q
-    outer = jnp.clip(outer, 0, width - 1)
+    outer = jnp.clip(jnp.where(place < 0, place + 32, place - width), 0, 31)
     inside = (place >= 0) & (place < width)
+
+    def all_rows(x, k):
+        return jnp.broadcast_to(x[k : k + 1], (8, width))
+
+    inner = [all_rows(inner, k) for k in range(4)]
+    outer = [all_rows(outer, k) for k in range(4)]
+    inside = [all_rows(inside, k) for k in range(4)]
 
     def pick(values, index):
         return jnp.take_along_axis(values, index, axis=1, mode="promise_in_bounds")
@@ -318,31 +355,35 @@
     g_south = jnp.where(sub < 4, -1.0, -g1)
     g_north = jnp.where(sub < 4, g1, 1.0)
 
-    for h in range(2):
+    def write(f):
+        return pltpu.make_async_copy(done.at[f], out_hbm.at[f], sems.at[f])
+
+    def field(f, carry):
+        shift = 32 * (f // 2)
         for b in range(levels // 8):
             at = slice(8 * b, 8 * b + 8)
-            t = [tend_ref[h, c, at, :] for c in range(4)]
+            t = [tend_ref[f, c, at, :] for c in range(4)]
             mean = 0.25 * ((t[0] + t[1]) + (t[2] + t[3]))
+            halo_at = pl.ds(pl.multiple_of((f % 2) * levels + 8 * b, 8), 8)
+            halos = (low_ref[halo_at, :], high_ref[halo_at, :])
             near = []
-            halo_at = slice(h * levels + 8 * b, h * levels + 8 * b + 8)
             for k in range(4):
-                halo = (low_ref if k % 2 == 0 else high_ref)[halo_at, :]
-                own_pick = pick(mean, jnp.broadcast_to(inner[k : k + 1], (8, width)))
-                halo_pick = pick(halo, jnp.broadcast_to(outer[k : k + 1], (8, width)))
-                near.append(
-                    jnp.where(jnp.broadcast_to(inside[k : k + 1], (8, width)), own_pick, halo_pick)
-                )
+                if k < 2:
+                    own_pick = pltpu.roll(mean, 1 if k == 0 else width - 1, 1)
+                else:
+                    own_pick = pick(mean, inner[k])
+                halo_pick = pick(halos[k % 2], outer[k] + shift)
+                near.append(jnp.where(inside[k], own_pick, halo_pick))
             low = functools.reduce(jnp.minimum, t + near)
             high = functools.reduce(jnp.maximum, t + near)
             slope_x = 0.5 * ((t[1] + t[3]) - (t[0] + t[2]))
             slope_y = 0.5 * ((t[2] + t[3]) - (t[0] + t[1]))
-            cross = (t[3] - t[2]) - (t[1] - t[0])
             scratch[0, at, :] = mean
             scratch[1, at, :] = slope_x - 0.5 * (near[0] - mean)
             scratch[2, at, :] = slope_x + 0.5 * (near[1] - mean)
             scratch[3, at, :] = slope_y - 0.5 * (near[2] - mean)
             scratch[4, at, :] = slope_y + 0.5 * (near[3] - mean)
-            scratch[5, at, :] = cross
+            scratch[5, at, :] = (t[3] - t[2]) - (t[1] - t[0])
             scratch[6, at, :] = low
             scratch[7, at, :] = high
         for l in range(levels):
@@ -351,21 +392,27 @@
             )
             base = mean + g_i * jnp.where(west_side, x_west, x_east)
             twist = g_i * cross
-            out_ref[h, l, 0:8, :] = jnp.minimum(
+            done[f, l, 0:8, :] = jnp.minimum(
                 jnp.maximum(base + g_south * (y_south + twist), low), high
             )
-            out_ref[h, l, 8:16, :] = jnp.minimum(
+            done[f, l, 8:16, :] = jnp.minimum(
                 jnp.maximum(base + g_north * (y_north + twist), low), high
             )
-
-
-def on_device(n_grp, n_row, n_x, gll_state, metric, phys_owner, neighbours, rate, forcing, mix):
+        write(f).start()
+        return carry
+
+    lax.fori_loop(0, fields, field, 0)
+    for f in range(fields):
+        write(f).wait()
+
+
+def on_device(n_grp, n_row, gll_state, metric, phys_owner, neighbours, rate, forcing, mix):
     fields, levels, nodes, elems = gll_state.shape
     slots = rate.shape[1]
-    hbm = pl.BlockSpec(memory_space=pl.ANY)
+    hbm = pl.BlockSpec(memory_space=pltpu.HBM)
     vmem = pl.BlockSpec(memory_space=pltpu.VMEM)
     tend, low, high = pl.pallas_call(
-        functools.partial(exchange_kernel, n_grp, n_row, n_x),
+        functools.partial(exchange_kernel, n_grp, n_row),
         out_shape=(
             jax.ShapeDtypeStruct((fields, 4, levels, elems), F32),
             jax.ShapeDtypeStruct((2 * levels, elems), F32),
@@ -391,33 +438,41 @@
             pltpu.VMEM((2, 2 * levels, elems), F32),
             pltpu.SemaphoreType.DMA((5,)),
             pltpu.SemaphoreType.DMA((fields,)),
-            pltpu.SemaphoreType.DMA((n_grp - 1,)),
-            pltpu.SemaphoreType.DMA((n_grp - 1,)),
+            pltpu.SemaphoreType.DMA((n_grp,)),
+            pltpu.SemaphoreType.DMA((n_grp,)),
             pltpu.SemaphoreType.DMA((2,)),
             pltpu.SemaphoreType.DMA((2,)),
+            pltpu.SemaphoreType.REGULAR((n_grp,)),
+            pltpu.SemaphoreType.REGULAR((2,)),
         ],
-        compiler_params=pltpu.CompilerParams(collective_id=0, has_side_effects=True),
+        compiler_params=pltpu.CompilerParams(
+            collective_id=0, has_side_effects=True, vmem_limit_bytes=16 << 20
+        ),
         name="exchange",
     )(
-        gll_state.reshape(fields, levels * nodes, elems),
-        metric,
-        phys_owner[:, :, 0].T,
-        rate,
-        forcing,
-        mix,
+        *(
+            pltpu.with_memory_space_constraint(x, pltpu.HBM)
+            for x in (
+                gll_state.reshape(fields, levels * nodes, elems),
+                metric,
+                phys_owner[:, :, 0].T,
+                rate,
+                forcing,
+                mix,
+            )
+        )
     )
     return pl.pallas_call(
         functools.partial(nodes_kernel, elems * n_grp * n_row, n_row),
-        grid=(fields // 2,),
         out_shape=jax.ShapeDtypeStruct(gll_state.shape, F32),
-        in_specs=[
-            pl.BlockSpec((2, 4, levels, elems), lambda i: (i, 0, 0, 0)),
-            pl.BlockSpec((2 * levels, elems), lambda i: (0, 0)),
-            pl.BlockSpec((2 * levels, elems), lambda i: (0, 0)),
-            pl.BlockSpec((4, elems), lambda i: (0, 0)),
+        in_specs=[vmem] * 4,
+        out_specs=hbm,
+        scratch_shapes=[
+            pltpu.VMEM((fields, levels, nodes, elems), F32),
+            pltpu.VMEM((8, levels, elems), F32),
+            pltpu.SemaphoreType.DMA((fields,)),
         ],
-        out_specs=pl.BlockSpec((2, levels, nodes, elems), lambda i: (i, 0, 0, 0)),
-        scratch_shapes=[pltpu.VMEM((8, levels, elems), F32)],
+        compiler_params=pltpu.CompilerParams(vmem_limit_bytes=16 << 20),
         name="nodes",
     )(tend, low, high, neighbours)
 
@@ -435,7 +490,7 @@
     out_specs = P(None, None, None, ("grp", "row"))
     n_grp, n_row = mesh.shape["grp"], mesh.shape["row"]
     return jax.shard_map(
-        functools.partial(on_device, n_grp, n_row, 4),
+        functools.partial(on_device, n_grp, n_row),
         mesh=mesh,
         in_specs=in_specs,
         out_specs=out_specs,

time: 39.9 us -> 33.7 us (0.84)
  the two profiles are of different devices: /device:TPU:25 before, /device:TPU:128 now
where the time goes in v2:
time: 33.7 us; the launch traced here: 33.6 us
  Pallas kernels  33.6 us (100%)
    pallas_call x1, Pallas kernels, on_device(): pl.pallas_call(functools.partial(exchange_kernel, n_grp, n_row), out_shap...  31.2 us
    pallas_call x1, Pallas kernels, on_device(): pl.pallas_call(functools.partial(nodes_kernel, elems * n_grp * n_row, n_r...  2.31 us

profile of v2, /device:TPU:128, one launch (start us, length us, event | category | flops | bytes accessed | tf_op | source)
XLA Modules:
  0.0 33.6 jit_solution(17387743910860850206)
XLA Ops:
  0.0 0.0 copy-start
  0.0 31.2 %exchange.1 = (f32[8,4,32,128]{3,2,1,0:T(8,128)S(1)}, f32[64,128]{1,0:T(8,128)S(1)}, f32[64,128]{1,0:T(8,128)S(1)}) custom-call(f32[8,512,128]{2,1,0:T(8,128)} %bitcast.4, f32[16,128]{1,0:T(8,128)} %metric_hbm.1, s32[4,128]{1,0:T(4,128)} %bitcast.5, f32[32,1056]{1,0:T(8,128)} %rate_hbm.1, f32[32,1056]{1,0:T(8,128)} %forcing_hbm.1, f32[8,8]{1,0:T(8,128)} %mix_hbm.1), custom_call_target="tpu_custom_call" | custom-call | tf_op jit(solution)/shard_map/exchange/pallas_call | solution.py:414
  31.3 0.0 copy-done
  31.3 2.3 %nodes.1 = f32[8,32,16,128]{3,2,1,0:T(8,128)} custom-call(f32[8,4,32,128]{3,2,1,0:T(8,128)S(1)} %get-tuple-element.8.tend_ref, f32[64,128]{1,0:T(8,128)S(1)} %get-tuple-element.9.low_ref, f32[64,128]{1,0:T(8,128)S(1)} %get-tuple-element.10.high_ref, s32[4,128]{1,0:T(4,128)S(1)} %copy-done), custom_call_target="tpu_custom_call" | custom-call | tf_op jit(solution)/shard_map/nodes/pallas_call | solution.py:465
Async XLA Ops:
  0.0 31.3 %copy-start = (s32[4,128]{1,0:T(4,128)S(1)}, s32[4,128]{1,0:T(4,128)}, u32[]{:S(2)}) copy-start(s32[4,128]{1,0:T(4,128)} %near_ref.1) | copy-start | bytes 6148

commit v3 on v2

--- a/solution.py
+++ b/solution.py
@@ -44,6 +44,7 @@
 def exchange_kernel(
     n_grp,
     n_row,
+    n_x,
     gll_hbm,
     metric_hbm,
     owner_hbm,
@@ -69,9 +70,8 @@
     edge_out,
     edge_in,
     in_sem,
-    gll_sem,
-    send_sem,
-    recv_sem,
+    sent,
+    came,
     edge_send_sem,
     edge_recv_sem,
     ready,
@@ -80,6 +80,8 @@
     fields = gll_hbm.shape[0]
     me = lax.axis_index("grp")
     my_row = lax.axis_index("row")
+    n_z = n_grp // n_x
+    my_z, my_x = me // n_x, me % n_x
 
     small = [
         pltpu.make_async_copy(src, dst, in_sem.at[k])
@@ -95,12 +97,7 @@
     ]
     for copy in small:
         copy.start()
-    gll_copies = [
-        pltpu.make_async_copy(gll_hbm.at[f], gbuf.at[f], gll_sem.at[f]) for f in range(fields)
-    ]
-    for copy in gll_copies:
-        copy.start()
-
+    gll_copy = pltpu.make_async_copy(gll_hbm, gbuf, in_sem.at[5])
     here = me * n_row + my_row
     total = n_grp * n_row
     after = lax.rem(here + 1, total)
@@ -115,16 +112,19 @@
 
     lax.fori_loop(me + 1, n_grp, greet, 0)
 
-    @pl.when(here < total - 1)
+    @pl.when(my_row < n_row - 1)
     def _():
         pl.semaphore_signal(barrier, inc=1, device_id=sides[1], device_id_type=MESH)
 
-    @pl.when(here == 0)
+    @pl.when(my_row == 0)
     def _():
         pl.semaphore_signal(barrier, inc=1, device_id=sides[0], device_id_type=MESH)
+
+    beside = jnp.where(my_row > 0, 1, 0) + jnp.where(my_row == n_row - 1, 1, 0)
 
     small[0].wait()
     small[1].wait()
+    gll_copy.start()
     slot_count = rate_ref.shape[1]
     for k in range(0, slot_count, 128):
         width = min(128, slot_count - k)
@@ -136,41 +136,45 @@
         at = 2 * HIGH * g
         send[g] = jnp.where(lane < 64, slots_t[at : at + HIGH], slots_t[at + HIGH : at + 2 * HIGH])
 
-    below = jnp.where(here > 0, 1, 0) + jnp.where(here == total - 1, 1, 0)
-
     @pl.when(here > 0)
     def _():
-        pl.semaphore_wait(barrier, me + below)
+        pl.semaphore_wait(barrier, me + beside)
+
+    @pl.when(my_row > 0)
+    def _():
+        pl.semaphore_signal(edge_ready.at[1], inc=1, device_id=sides[0], device_id_type=MESH)
+
+    @pl.when(my_row == n_row - 1)
+    def _():
+        pl.semaphore_signal(edge_ready.at[0], inc=1, device_id=sides[1], device_id_type=MESH)
 
     def block_copy(there, origin):
         return pltpu.make_async_remote_copy(
             src_ref=send.at[there],
             dst_ref=recv.at[me],
-            send_sem=send_sem.at[there],
-            recv_sem=recv_sem.at[origin],
+            send_sem=sent,
+            recv_sem=came.at[origin],
             device_id=(there, my_row),
             device_id_type=MESH,
         )
 
-    def send_down(g, carry):
-        block_copy(g, me).start()
-        return carry
-
-    lax.fori_loop(0, me, send_down, 0)
-
-    def tell(g, carry):
-        pl.semaphore_signal(ready.at[me], inc=1, device_id=(g, my_row), device_id_type=MESH)
-        return carry
-
-    lax.fori_loop(0, me, tell, 0)
-
-    @pl.when(here > 0)
-    def _():
-        pl.semaphore_signal(edge_ready.at[1], inc=1, device_id=sides[0], device_id_type=MESH)
-
-    @pl.when(here == total - 1)
-    def _():
-        pl.semaphore_signal(edge_ready.at[0], inc=1, device_id=sides[1], device_id_type=MESH)
+    def tell(g):
+        pl.semaphore_signal(ready.at[my_z], inc=1, device_id=(g, my_row), device_id_type=MESH)
+
+    def send_down(z, carry):
+        for x in range(n_x):
+            tell(z * n_x + x)
+            block_copy(z * n_x + x, my_z).start()
+        return carry
+
+    lax.fori_loop(0, my_z, send_down, 0)
+
+    def send_beside(g, carry):
+        tell(g)
+        block_copy(g, my_z).start()
+        return carry
+
+    lax.fori_loop(my_z * n_x, me, send_beside, 0)
 
     small[2].wait()
     table = cell_weights()
@@ -182,8 +186,7 @@
             wbuf[16 * c + n : 16 * c + n + 1, :] = weighted[n] * inverse
 
     levels = tend_ref.shape[2]
-    for copy in gll_copies:
-        copy.wait()
+    gll_copy.wait()
 
     def to_cells(f, carry):
         sums = [None] * 4
@@ -196,7 +199,8 @@
             cells[f, c] = sums[c]
         return carry
 
-    lax.fori_loop(0, fields, to_cells, 0)
+    lax.fori_loop(0, fields // 2, to_cells, 0)
+    lax.fori_loop(fields // 2, fields, to_cells, 0)
 
     small[4].wait()
 
@@ -241,21 +245,47 @@
     rows[...] = jnp.zeros_like(rows)
     recv[me] = send[me]
 
-    def send_up(g, carry):
-        pl.semaphore_wait(ready.at[g], 1)
-        block_copy(g, me).start()
-        return carry
-
-    lax.fori_loop(me + 1, n_grp, send_up, 0)
+    @pl.when(my_x < n_x - 1)
+    def _():
+        pl.semaphore_wait(ready.at[my_z], n_x - 1 - my_x)
+
+    def start_up(g, carry):
+        block_copy(g, my_z).start()
+        return carry
+
+    lax.fori_loop(me + 1, (my_z + 1) * n_x, start_up, 0)
+
+    def send_up(z, carry):
+        pl.semaphore_wait(ready.at[z], n_x)
+        for x in range(n_x):
+            block_copy(z * n_x + x, my_z).start()
+        return carry
+
+    lax.fori_loop(my_z + 1, n_z, send_up, 0)
+
+    def bytes_of(what, sem):
+        return pltpu.make_async_remote_copy(
+            src_ref=what,
+            dst_ref=what,
+            send_sem=sem,
+            recv_sem=sem,
+            device_id=sides[0],
+            device_id_type=MESH,
+        )
 
     picked = None
-    for k in range(n_grp // 16):
+    for k in range(n_z // 4):
+        for z in range(4 * k, 4 * k + 4):
+
+            @pl.when(z != my_z)
+            def _():
+                bytes_of(recv.at[pl.ds(0, n_x)], came.at[z]).wait_recv()
+
+            @pl.when(z == my_z)
+            def _():
+                bytes_of(recv.at[pl.ds(0, n_x - 1)], came.at[z]).wait_recv()
+
         for g in range(16 * k, 16 * k + 16):
-
-            @pl.when(g != me)
-            def _():
-                block_copy(me, g).wait_recv()
-
             rows[16 * g : 16 * g + HIGH, :] = recv[g]
         block = rows[256 * k : 256 * k + 256, :].T
         top = block.astype(BF16)
@@ -298,25 +328,19 @@
         for k in range(2)
     ]
 
-    @pl.when(here == 0)
+    @pl.when(my_row == 0)
     def _():
         pl.semaphore_wait(edge_ready.at[0], 1)
 
-    @pl.when(here < total - 1)
+    @pl.when(my_row < n_row - 1)
     def _():
         pl.semaphore_wait(edge_ready.at[1], 1)
 
     for copy in edge_copies:
         copy.start()
 
-    def sent(g, carry):
-        @pl.when(g != me)
-        def _():
-            block_copy(g, me).wait_send()
-
-        return carry
-
-    lax.fori_loop(0, n_grp, sent, 0)
+    bytes_of(send.at[pl.ds(0, n_grp - 1)], sent).wait_send()
+
     for copy in edge_copies:
         copy.wait()
     low_ref[...] = edge_in[0]
@@ -406,13 +430,13 @@
         write(f).wait()
 
 
-def on_device(n_grp, n_row, gll_state, metric, phys_owner, neighbours, rate, forcing, mix):
+def on_device(n_grp, n_row, n_x, gll_state, metric, phys_owner, neighbours, rate, forcing, mix):
     fields, levels, nodes, elems = gll_state.shape
-    slots = rate.shape[1]
+    slots, n_z = rate.shape[1], n_grp // n_x
     hbm = pl.BlockSpec(memory_space=pltpu.HBM)
     vmem = pl.BlockSpec(memory_space=pltpu.VMEM)
     tend, low, high = pl.pallas_call(
-        functools.partial(exchange_kernel, n_grp, n_row),
+        functools.partial(exchange_kernel, n_grp, n_row, n_x),
         out_shape=(
             jax.ShapeDtypeStruct((fields, 4, levels, elems), F32),
             jax.ShapeDtypeStruct((2 * levels, elems), F32),
@@ -436,13 +460,12 @@
             pltpu.VMEM((fields, 4, levels, elems), F32),
             pltpu.VMEM((2, 2 * levels, elems), F32),
             pltpu.VMEM((2, 2 * levels, elems), F32),
-            pltpu.SemaphoreType.DMA((5,)),
-            pltpu.SemaphoreType.DMA((fields,)),
-            pltpu.SemaphoreType.DMA((n_grp,)),
-            pltpu.SemaphoreType.DMA((n_grp,)),
+            pltpu.SemaphoreType.DMA((6,)),
+            pltpu.SemaphoreType.DMA,
+            pltpu.SemaphoreType.DMA((n_z,)),
             pltpu.SemaphoreType.DMA((2,)),
             pltpu.SemaphoreType.DMA((2,)),
-            pltpu.SemaphoreType.REGULAR((n_grp,)),
+            pltpu.SemaphoreType.REGULAR((n_z,)),
             pltpu.SemaphoreType.REGULAR((2,)),
         ],
         compiler_params=pltpu.CompilerParams(
@@ -490,7 +513,7 @@
     out_specs = P(None, None, None, ("grp", "row"))
     n_grp, n_row = mesh.shape["grp"], mesh.shape["row"]
     return jax.shard_map(
-        functools.partial(on_device, n_grp, n_row),
+        functools.partial(on_device, n_grp, n_row, 4),
         mesh=mesh,
         in_specs=in_specs,
         out_specs=out_specs,

time: 33.7 us -> 32.6 us (0.967)
  the two profiles are of different devices: /device:TPU:128 before, /device:TPU:64 now
where the time goes in v3:
time: 32.6 us; the launch traced here: 32.4 us
  Pallas kernels  32.4 us (99%)
    pallas_call x1, Pallas kernels, on_device(): pl.pallas_call(functools.partial(exchange_kernel, n_grp, n_row, n_x), out...  30.1 us
    pallas_call x1, Pallas kernels, on_device(): pl.pallas_call(functools.partial(nodes_kernel, elems * n_grp * n_row, n_r...  2.31 us

profile of v3, /device:TPU:64, one launch (start us, length us, event | category | flops | bytes accessed | tf_op | source)
XLA Modules:
  0.0 32.4 jit_solution(6865114148356759615)
XLA Ops:
  0.0 0.0 copy-start
  0.0 30.1 %exchange.1 = (f32[8,4,32,128]{3,2,1,0:T(8,128)S(1)}, f32[64,128]{1,0:T(8,128)S(1)}, f32[64,128]{1,0:T(8,128)S(1)}) custom-call(f32[8,512,128]{2,1,0:T(8,128)} %bitcast.4, f32[16,128]{1,0:T(8,128)} %metric_hbm.1, s32[4,128]{1,0:T(4,128)} %bitcast.5, f32[32,1056]{1,0:T(8,128)} %rate_hbm.1, f32[32,1056]{1,0:T(8,128)} %forcing_hbm.1, f32[8,8]{1,0:T(8,128)} %mix_hbm.1), custom_call_target="tpu_custom_call" | custom-call | tf_op jit(solution)/shard_map/exchange/pallas_call | solution.py:438
  30.1 0.0 copy-done
  30.1 2.3 %nodes.1 = f32[8,32,16,128]{3,2,1,0:T(8,128)} custom-call(f32[8,4,32,128]{3,2,1,0:T(8,128)S(1)} %get-tuple-element.8.tend_ref, f32[64,128]{1,0:T(8,128)S(1)} %get-tuple-element.9.low_ref, f32[64,128]{1,0:T(8,128)S(1)} %get-tuple-element.10.high_ref, s32[4,128]{1,0:T(4,128)S(1)} %copy-done), custom_call_target="tpu_custom_call" | custom-call | tf_op jit(solution)/shard_map/nodes/pallas_call | solution.py:488
Async XLA Ops:
  0.0 30.1 %copy-start = (s32[4,128]{1,0:T(4,128)S(1)}, s32[4,128]{1,0:T(4,128)}, u32[]{:S(2)}) copy-start(s32[4,128]{1,0:T(4,128)} %near_ref.1) | copy-start | bytes 6148

commit v4 on v3

--- a/solution.py
+++ b/solution.py
@@ -82,6 +82,7 @@
     my_row = lax.axis_index("row")
     n_z = n_grp // n_x
     my_z, my_x = me // n_x, me % n_x
+    around = [(my_x + d) % n_x for d in (2, 1, 3, 0)]
 
     small = [
         pltpu.make_async_copy(src, dst, in_sem.at[k])
@@ -95,7 +96,7 @@
             )
         )
     ]
-    for copy in small:
+    for copy in small[:2]:
         copy.start()
     gll_copy = pltpu.make_async_copy(gll_hbm, gbuf, in_sem.at[5])
     here = me * n_row + my_row
@@ -124,6 +125,8 @@
 
     small[0].wait()
     small[1].wait()
+    for copy in small[2:]:
+        copy.start()
     gll_copy.start()
     slot_count = rate_ref.shape[1]
     for k in range(0, slot_count, 128):
@@ -162,7 +165,7 @@
         pl.semaphore_signal(ready.at[my_z], inc=1, device_id=(g, my_row), device_id_type=MESH)
 
     def send_down(z, carry):
-        for x in range(n_x):
+        for x in around:
             tell(z * n_x + x)
             block_copy(z * n_x + x, my_z).start()
         return carry
@@ -257,7 +260,7 @@
 
     def send_up(z, carry):
         pl.semaphore_wait(ready.at[z], n_x)
-        for x in range(n_x):
+        for x in around:
             block_copy(z * n_x + x, my_z).start()
         return carry
 
@@ -348,7 +351,7 @@
 
 
 def nodes_kernel(
-    elems_total, n_row, tend_ref, low_ref, high_ref, near_ref, out_hbm, done, scratch, sems
+    elems_total, n_row, tend_ref, low_ref, high_ref, near_ref, out_hbm, done, scratch, sem
 ):
     fields, _, levels, width = tend_ref.shape
     here = (lax.axis_index("grp") * n_row + lax.axis_index("row")) * width
@@ -380,7 +383,7 @@
     g_north = jnp.where(sub < 4, g1, 1.0)
 
     def write(f):
-        return pltpu.make_async_copy(done.at[f], out_hbm.at[f], sems.at[f])
+        return pltpu.make_async_copy(done.at[f], out_hbm.at[f], sem)
 
     def field(f, carry):
         shift = 32 * (f // 2)
@@ -426,8 +429,7 @@
         return carry
 
     lax.fori_loop(0, fields, field, 0)
-    for f in range(fields):
-        write(f).wait()
+    pltpu.make_async_copy(done, out_hbm, sem).wait()
 
 
 def on_device(n_grp, n_row, n_x, gll_state, metric, phys_owner, neighbours, rate, forcing, mix):
@@ -493,7 +495,7 @@
         scratch_shapes=[
             pltpu.VMEM((fields, levels, nodes, elems), F32),
             pltpu.VMEM((8, levels, elems), F32),
-            pltpu.SemaphoreType.DMA((fields,)),
+            pltpu.SemaphoreType.DMA,
         ],
         compiler_params=pltpu.CompilerParams(vmem_limit_bytes=16 << 20),
         name="nodes",

time: 32.6 us -> 32.5 us (level)
  no operation moved by 1% of the time
where the time goes in v4:
time: 32.5 us; the launch traced here: 32.4 us
  Pallas kernels  32.3 us (99%)
    pallas_call x1, Pallas kernels, on_device(): pl.pallas_call(functools.partial(exchange_kernel, n_grp, n_row, n_x), out...  30.1 us
    pallas_call x1, Pallas kernels, on_device(): pl.pallas_call(functools.partial(nodes_kernel, elems * n_grp * n_row, n_r...  2.25 us

profile of v4, /device:TPU:64, one launch (start us, length us, event | category | flops | bytes accessed | tf_op | source)
XLA Modules:
  0.0 32.4 jit_solution(13964821032636819745)
XLA Ops:
  0.0 0.0 copy-start
  0.0 30.1 %exchange.1 = (f32[8,4,32,128]{3,2,1,0:T(8,128)S(1)}, f32[64,128]{1,0:T(8,128)S(1)}, f32[64,128]{1,0:T(8,128)S(1)}) custom-call(f32[8,512,128]{2,1,0:T(8,128)} %bitcast.4, f32[16,128]{1,0:T(8,128)} %metric_hbm.1, s32[4,128]{1,0:T(4,128)} %bitcast.5, f32[32,1056]{1,0:T(8,128)} %rate_hbm.1, f32[32,1056]{1,0:T(8,128)} %forcing_hbm.1, f32[8,8]{1,0:T(8,128)} %mix_hbm.1), custom_call_target="tpu_custom_call" | custom-call | tf_op jit(solution)/shard_map/exchange/pallas_call | solution.py:440
  30.1 0.0 copy-done
  30.1 2.2 %nodes.1 = f32[8,32,16,128]{3,2,1,0:T(8,128)} custom-call(f32[8,4,32,128]{3,2,1,0:T(8,128)S(1)} %get-tuple-element.8.tend_ref, f32[64,128]{1,0:T(8,128)S(1)} %get-tuple-element.9.low_ref, f32[64,128]{1,0:T(8,128)S(1)} %get-tuple-element.10.high_ref, s32[4,128]{1,0:T(4,128)S(1)} %copy-done), custom_call_target="tpu_custom_call" | custom-call | tf_op jit(solution)/shard_map/nodes/pallas_call | solution.py:490
Async XLA Ops:
  0.0 30.1 %copy-start = (s32[4,128]{1,0:T(4,128)S(1)}, s32[4,128]{1,0:T(4,128)}, u32[]{:S(2)}) copy-start(s32[4,128]{1,0:T(4,128)} %near_ref.1) | copy-start | bytes 6148

commit v5 on v4

--- a/solution.py
+++ b/solution.py
@@ -382,8 +382,11 @@
     g_south = jnp.where(sub < 4, -1.0, -g1)
     g_north = jnp.where(sub < 4, g1, 1.0)
 
-    def write(f):
-        return pltpu.make_async_copy(done.at[f], out_hbm.at[f], sem)
+    half = levels // 2
+
+    def write(f, k):
+        part = pl.ds(half * k, half)
+        return pltpu.make_async_copy(done.at[f, part], out_hbm.at[f, part], sem)
 
     def field(f, carry):
         shift = 32 * (f // 2)
@@ -425,7 +428,8 @@
             done[f, l, 8:16, :] = jnp.minimum(
                 jnp.maximum(base + g_north * (y_north + twist), low), high
             )
-        write(f).start()
+            if l % half == half - 1:
+                write(f, l // half).start()
         return carry
 
     lax.fori_loop(0, fields, field, 0)

time: 32.5 us -> 32.5 us (level)
  no operation moved by 1% of the time
where the time goes in v5:
time: 32.5 us; the launch traced here: 32.3 us
  Pallas kernels  32.3 us (99%)
    pallas_call x1, Pallas kernels, on_device(): pl.pallas_call(functools.partial(exchange_kernel, n_grp, n_row, n_x), out...  30.1 us
    pallas_call x1, Pallas kernels, on_device(): pl.pallas_call(functools.partial(nodes_kernel, elems * n_grp * n_row, n_r...  2.21 us

profile of v5, /device:TPU:64, one launch (start us, length us, event | category | flops | bytes accessed | tf_op | source)
XLA Modules:
  0.0 32.3 jit_solution(7183457996090904517)
XLA Ops:
  0.0 0.0 copy-start
  0.0 30.1 %exchange.1 = (f32[8,4,32,128]{3,2,1,0:T(8,128)S(1)}, f32[64,128]{1,0:T(8,128)S(1)}, f32[64,128]{1,0:T(8,128)S(1)}) custom-call(f32[8,512,128]{2,1,0:T(8,128)} %bitcast.4, f32[16,128]{1,0:T(8,128)} %metric_hbm.1, s32[4,128]{1,0:T(4,128)} %bitcast.5, f32[32,1056]{1,0:T(8,128)} %rate_hbm.1, f32[32,1056]{1,0:T(8,128)} %forcing_hbm.1, f32[8,8]{1,0:T(8,128)} %mix_hbm.1), custom_call_target="tpu_custom_call" | custom-call | tf_op jit(solution)/shard_map/exchange/pallas_call | solution.py:444
  30.1 0.0 copy-done
  30.1 2.2 %nodes.1 = f32[8,32,16,128]{3,2,1,0:T(8,128)} custom-call(f32[8,4,32,128]{3,2,1,0:T(8,128)S(1)} %get-tuple-element.8.tend_ref, f32[64,128]{1,0:T(8,128)S(1)} %get-tuple-element.9.low_ref, f32[64,128]{1,0:T(8,128)S(1)} %get-tuple-element.10.high_ref, s32[4,128]{1,0:T(4,128)S(1)} %copy-done), custom_call_target="tpu_custom_call" | custom-call | tf_op jit(solution)/shard_map/nodes/pallas_call | solution.py:494
Async XLA Ops:
  0.0 30.1 %copy-start = (s32[4,128]{1,0:T(4,128)S(1)}, s32[4,128]{1,0:T(4,128)}, u32[]{:S(2)}) copy-start(s32[4,128]{1,0:T(4,128)} %near_ref.1) | copy-start | bytes 6148
